TPU v7x, 32 devices: a whole 2x2x4 slice. The times are simulated.
32 devices in a mesh: freq: 16 (over z, y, x), rhalf: 2 (over core).
Axes of the slice: x: 2, y: 2, z: 4, core: 2. Of those that a mesh axis runs over, the one named last changes fastest.
Arguments:
- reflection: bfloat16 [32, 2, 2048, 2048], P('freq', None, None, 'rhalf'), may hold values from -1 to 1, as said below
- focusing_direct: bfloat16 [2048, 2, 32, 128], P('rhalf', None, 'freq'), may hold values from -6 to 6
- arrival_index: int32 [2048, 128], P('rhalf'), may hold values from 8 to 23
Outputs:
- green: bfloat16 [128, 2048, 64], P('freq', 'rhalf')
Inputs may be any that keep to these rules, and one draw needn't show every extreme that they name: For every frequency and part, reflection[k, c] is a symmetric 2048 x 2048 matrix (reciprocity).
All inputs are finite; a program needn't handle non-finite values.
Results may differ from a plain program's by a relative error of at most 0.017.
Values may be sent and summed in bfloat16 or wider, within the bound.
A program may use at most 64 MiB of HBM per device.

v0:
```python
import math

import jax
import jax.numpy as jnp
from jax import lax
from jax.sharding import PartitionSpec as P


def transform_tables(nfreq):
    ntime = 2 * nfreq
    freqs = jnp.arange(nfreq, dtype=jnp.int32)
    times = jnp.arange(ntime, dtype=jnp.int32)
    phases = freqs[:, None] * times[None, :] % ntime
    angles = phases.astype(jnp.float32) * (2.0 * math.pi / ntime)
    norm_factor = 1.0 / math.sqrt(ntime)
    weights = jnp.where(freqs == 0, 1.0, 2.0).astype(jnp.float32)[:, None] * norm_factor
    inverse = jnp.stack([weights * jnp.cos(angles), -weights * jnp.sin(angles)])
    forward = jnp.stack([jnp.cos(angles).T, -jnp.sin(angles).T]) * norm_factor
    return (inverse, forward)


def pass_window(arrival, ntime):
    times = jnp.arange(ntime, dtype=jnp.int32)
    shifted = jnp.where(times < ntime // 2, times, times - ntime)
    return (jnp.abs(shifted)[None, :, None] < arrival[:, None, :]).astype(jnp.float32)


def combine(products, signed):
    real_part = products[:, 0, :, 0] - signed * products[:, 1, :, 1]
    imag_part = products[:, 0, :, 1] + signed * products[:, 1, :, 0]
    return jnp.stack([real_part, imag_part], axis=1)


def per_device(reflection, focusing_direct, arrival_index):
    quarter_rows = focusing_direct.shape[0]
    freq_local = focusing_direct.shape[2]
    points = focusing_direct.shape[3]
    freq_devices = lax.axis_size("freq")
    nfreq = freq_local * freq_devices
    ntime = 2 * nfreq
    inverse, forward = transform_tables(nfreq)
    owned_rows = quarter_rows // freq_devices
    my_index = lax.axis_index("freq")
    owned_arrival = lax.dynamic_slice_in_dim(arrival_index, my_index * owned_rows, owned_rows, 0)
    window = pass_window(owned_arrival, ntime)

    def reflect(field, signed):
        products = jnp.einsum(
            "fasr,rbfp->safbp", reflection, field, preferred_element_type=jnp.float32
        )
        return lax.psum_scatter(
            combine(products, signed).astype(jnp.bfloat16), "rhalf", scatter_dimension=0, tiled=True
        ).astype(jnp.float32)

    def mute(spectra):
        gathered = lax.all_to_all(
            spectra.astype(jnp.bfloat16), "freq", split_axis=0, concat_axis=2, tiled=True
        ).astype(spectra.dtype)
        signal = (
            jnp.einsum("rcfp,cft->rtp", gathered, inverse, precision=lax.Precision.HIGHEST) * window
        )
        back = jnp.einsum("rtp,ctf->rcfp", signal, forward, precision=lax.Precision.HIGHEST)
        return lax.all_to_all(
            back.astype(jnp.bfloat16), "freq", split_axis=2, concat_axis=0, tiled=True
        ).astype(back.dtype)

    minus = mute(reflect(focusing_direct, 1.0)).astype(jnp.bfloat16)
    plus = (focusing_direct.astype(jnp.float32) + mute(reflect(minus, -1.0))).astype(jnp.bfloat16)
    upgoing = reflect(plus, 1.0)
    points_here = points // freq_devices
    regrouped = lax.all_to_all(
        upgoing.astype(jnp.bfloat16), "freq", split_axis=3, concat_axis=2, tiled=True
    ).astype(upgoing.dtype)
    point_arrival = lax.dynamic_slice_in_dim(arrival_index, my_index * points_here, points_here, 1)
    outside = 1.0 - jnp.transpose(pass_window(point_arrival, ntime), (2, 0, 1))
    traces = jnp.einsum("rcfp,cft->prt", regrouped, inverse, precision=lax.Precision.HIGHEST)
    green = (traces * outside).astype(jnp.bfloat16)
    return green


def solution(mesh):
    return jax.shard_map(
        per_device,
        mesh=mesh,
        in_specs=(P("freq", None, None, "rhalf"), P("rhalf", None, "freq", None), P("rhalf", None)),
        out_specs=P("freq", "rhalf", None),
        check_vma=False,
    )
```

profile of v0, /device:TPU:8, one launch (start us, length us, event | category | flops | bytes accessed | tf_op | source)
XLA Modules:
  0.0 295.0 jit_solution(4237349779049489469)
XLA Ops:
  6.5 14.1 %fusion.6 = f32[2048,2,2,2,128]{0,4,1,3,2:T(8,128)} fusion(bf16[2,2,2048,1024]{3,2,1,0:T(8,128)(2,1)} %param.3, bf16[1024,2,2,128,1]{3,2,1,0,4:T(2,128)(2,1)} %bitcast.183), kind=kOutput, calls=%fused_computation.6 | convolution fusion | flops 4294967296 | bytes 26214400 | tf_op jit(solution)/shard_map/fasr,rbfp->safbp/dot_general | solution.py:48
  20.6 2.5 fusion.48
  23.1 2.5 fusion.49
  25.6 1.5 pad_maximum_fusion
  27.2 11.3 %reduce-scatter.4.cloned.1.call-done = bf16[1024,2,2,128]{0,3,2,1:T(8,128)(2,1)} async-done(((bf16[2048,2,2,128]{0,3,2,1:T(8,128)(2,1)}), bf16[1024,2,2,128]{0,3,2,1:T(8,128)(2,1)}) %reduce-scatter.4.cloned.1.call-update) | async-done | bytes 1048592 | tf_op jit(solution)/shard_map/reduce_scatter | solution.py:51
  38.5 3.7 %copy.62 = bf16[1024,2,2,128]{3,2,1,0:T(2,128)(2,1)} copy(bf16[1024,2,2,128]{0,3,2,1:T(8,128)(2,1)} %reduce-scatter.4.cloned.1.call-done) | data formatting | bytes 2097152 | tf_op jit(solution)/shard_map/reduce_scatter | solution.py:51
  42.1 7.0 %all-to-all-start = ((bf16[1024,2,2,128]{3,2,1,0:T(2,128)(2,1)}), bf16[1024,2,2,128]{3,2,1,0:T(2,128)(2,1)S(1)}, u32[]{:S(2)}, u32[]{:S(2)}) async-start(bf16[1024,2,2,128]{3,2,1,0:T(2,128)(2,1)} %copy.62), calls=%async_computation.1 | async-start | bytes 2097152 | tf_op jit(solution)/shard_map/all_to_all | solution.py:56
  49.2 0.1 sine_negate_fusion
  49.3 0.1 cosine_multiply_fusion
  49.4 0.1 sine_multiply_fusion
  49.5 25.4 %all-to-all-done = bf16[1024,2,2,128]{3,2,1,0:T(2,128)(2,1)S(1)} async-done(((bf16[1024,2,2,128]{3,2,1,0:T(2,128)(2,1)}), bf16[1024,2,2,128]{3,2,1,0:T(2,128)(2,1)S(1)}, u32[]{:S(2)}, u32[]{:S(2)}) %all-to-all-start) | async-done | bytes 1048608 | tf_op jit(solution)/shard_map/all_to_all | solution.py:56
  74.8 0.1 copy.63
  75.0 0.1 copy.64
  75.1 1.4 fusion.59
  76.5 1.9 fusion.42
  78.4 0.4 copy.66
  78.9 29.4 %all_to_all.81 = bf16[64,2,32,128]{3,0,1,2:T(8,128)(2,1)S(1)} all-to-all(bf16[64,2,32,128]{3,0,1,2:T(8,128)(2,1)S(1)} %copy.66), channel_id=1, replica_groups=mesh['freq'=16,'rhalf'=2] {'freq'}, dimensions={2} | all-to-all | bytes 2097152 | tf_op jit(solution)/shard_map/all_to_all | solution.py:63
  108.3 0.1 copy.68
  108.4 19.1 %fusion.9 = f32[2048,2,2,2,128]{0,4,1,3,2:T(8,128)} fusion(bf16[2,2,2048,1024]{3,2,1,0:T(8,128)(2,1)} %param.3, bf16[1024,2,2,128,1]{3,0,2,1,4:T(8,128)(2,1)S(1)} %bitcast.182), kind=kOutput, calls=%fused_computation.7 | convolution fusion | flops 4294967296 | bytes 26214400 | tf_op jit(solution)/shard_map/fasr,rbfp->safbp/dot_general | solution.py:48
  127.5 2.6 fusion.50
  130.1 2.6 fusion.51
  132.7 1.5 pad_maximum_fusion.1
  134.2 0.0 reduce-scatter.8.cloned.1.call-start
  134.3 8.6 %reduce-scatter.6.cloned.1.call-done = bf16[1024,2,2,128]{0,3,2,1:T(8,128)(2,1)} async-done(((bf16[2048,2,2,128]{0,3,2,1:T(8,128)(2,1)}), bf16[1024,2,2,128]{0,3,2,1:T(8,128)(2,1)}) %reduce-scatter.6.cloned.1.call-update) | async-done | bytes 1048592 | tf_op jit(solution)/shard_map/reduce_scatter | solution.py:51
  142.8 2.4 copy.73
  145.3 32.8 %all_to_all.82 = bf16[1024,2,2,128]{3,2,1,0:T(2,128)(2,1)S(1)} all-to-all(bf16[1024,2,2,128]{3,2,1,0:T(2,128)(2,1)S(1)} %copy.73), channel_id=1, replica_groups=mesh['freq'=16,'rhalf'=2] {'freq'}, dimensions={0} | all-to-all | bytes 2097152 | tf_op jit(solution)/shard_map/all_to_all | solution.py:56
  178.1 0.1 copy.74
  178.3 0.1 copy.75
  178.3 1.4 fusion.57
  179.8 1.9 fusion.45
  181.7 0.4 copy.77
  182.1 29.4 %all_to_all.83 = bf16[64,2,32,128]{3,0,1,2:T(8,128)(2,1)S(1)} all-to-all(bf16[64,2,32,128]{3,0,1,2:T(8,128)(2,1)S(1)} %copy.77), channel_id=1, replica_groups=mesh['freq'=16,'rhalf'=2] {'freq'}, dimensions={2} | all-to-all | bytes 2097152 | tf_op jit(solution)/shard_map/all_to_all | solution.py:63
  211.5 0.2 convert_bitcast_fusion
  211.7 1.6 copy.78
  213.4 1.2 fusion.35
  214.6 19.1 %fusion.12 = f32[2048,2,2,2,128]{0,4,1,3,2:T(8,128)} fusion(bf16[2,2,2048,1024]{3,2,1,0:T(8,128)(2,1)} %param.3, bf16[1024,2,2,128,1]{3,2,1,0,4:T(2,128)(2,1)S(1)} %bitcast.184), kind=kOutput, calls=%fused_computation.8 | convolution fusion | flops 4294967296 | bytes 26214400 | tf_op jit(solution)/shard_map/fasr,rbfp->safbp/dot_general | solution.py:48
  233.7 2.5 fusion.52
  236.2 2.5 fusion.53
  238.7 1.5 pad_maximum_fusion.2
  240.2 8.7 %reduce-scatter.8.cloned.1.call-done = bf16[1024,2,2,128]{0,3,2,1:T(8,128)(2,1)} async-done(((bf16[2048,2,2,128]{0,3,2,1:T(8,128)(2,1)}), bf16[1024,2,2,128]{0,3,2,1:T(8,128)(2,1)}) %reduce-scatter.8.cloned.1.call-update) | async-done | bytes 1048592 | tf_op jit(solution)/shard_map/reduce_scatter | solution.py:51
  248.9 3.3 %copy.82 = bf16[1024,2,2,128]{0,2,1,3:T(2,128)(2,1)} copy(bf16[1024,2,2,128]{0,3,2,1:T(8,128)(2,1)} %reduce-scatter.8.cloned.1.call-done) | data formatting | bytes 2097152 | tf_op jit(solution)/shard_map/reduce_scatter | solution.py:51
  252.2 7.0 %all-to-all-start.4 = ((bf16[1024,2,2,128]{0,2,1,3:T(2,128)(2,1)}), bf16[1024,2,2,128]{0,2,1,3:T(2,128)(2,1)S(1)}, u32[]{:S(2)}, u32[]{:S(2)}) async-start(bf16[1024,2,2,128]{0,2,1,3:T(2,128)(2,1)} %copy.82), calls=%async_computation.7 | async-start | bytes 2097152 | tf_op jit(solution)/shard_map/all_to_all | solution.py:71
  259.1 0.2 dynamic-slice_bitcast_fusion
  259.3 0.2 copy.84
  259.5 25.4 %all-to-all-done.4 = bf16[1024,2,2,128]{0,2,1,3:T(2,128)(2,1)S(1)} async-done(((bf16[1024,2,2,128]{0,2,1,3:T(2,128)(2,1)}), bf16[1024,2,2,128]{0,2,1,3:T(2,128)(2,1)S(1)}, u32[]{:S(2)}, u32[]{:S(2)}) %all-to-all-start.4) | async-done | bytes 1048608 | tf_op jit(solution)/shard_map/all_to_all | solution.py:71
  284.9 1.0 copy.117
  285.9 0.4 all_to_all.75
  286.3 2.1 fusion.32
  (12 shorter events, 0.1 us)
Async XLA Ops:
  6.5 42.7 %copy-start = (s32[1024,128]{1,0:T(8,128)S(1)}, s32[1024,128]{1,0:T(8,128)}, u32[]{:S(2)}) copy-start(s32[1024,128]{1,0:T(8,128)} %param.5) | copy-start | bytes 1572868
  6.5 31.9 %reduce-scatter.4.cloned.1.call-start = ((), (), s32[]{:S(2)}) async-start(), calls=%async_computation.8 | async-start | bytes 3145728 | tf_op jit(solution)/shard_map/reduce_scatter | solution.py:51
  42.1 32.7 %all-to-all-start = ((bf16[1024,2,2,128]{3,2,1,0:T(2,128)(2,1)}), bf16[1024,2,2,128]{3,2,1,0:T(2,128)(2,1)S(1)}, u32[]{:S(2)}, u32[]{:S(2)}) async-start(bf16[1024,2,2,128]{3,2,1,0:T(2,128)(2,1)} %copy.62), calls=%async_computation.1 | async-start | bytes 2097152 | tf_op jit(solution)/shard_map/all_to_all | solution.py:56
  49.1 93.7 %reduce-scatter.6.cloned.1.call-start = ((), (), s32[]{:S(2)}) async-start(), calls=%async_computation.9 | async-start | bytes 3145728 | tf_op jit(solution)/shard_map/reduce_scatter | solution.py:51
  134.2 114.7 %reduce-scatter.8.cloned.1.call-start = ((), (), s32[]{:S(2)}) async-start(), calls=%async_computation.10 | async-start | bytes 3145728 | tf_op jit(solution)/shard_map/reduce_scatter | solution.py:51
  211.7 1.6 copy-start.1
  252.2 32.7 %all-to-all-start.4 = ((bf16[1024,2,2,128]{0,2,1,3:T(2,128)(2,1)}), bf16[1024,2,2,128]{0,2,1,3:T(2,128)(2,1)S(1)}, u32[]{:S(2)}, u32[]{:S(2)}) async-start(bf16[1024,2,2,128]{0,2,1,3:T(2,128)(2,1)} %copy.82), calls=%async_computation.7 | async-start | bytes 2097152 | tf_op jit(solution)/shard_map/all_to_all | solution.py:71
Sparse Core Ops, SparseCore 0:
  27.3 11.1 reduce-scatter.3
  134.3 8.4 reduce-scatter.5
  240.3 8.5 reduce-scatter.7
where the time goes:
time: 296 us; the launch traced here: 295 us
  blocking collectives  91.6 us (31%)
  waiting for transfers between devices  79.4 us (27%)
  matrix products  61 us (21%)
  other arithmetic  21.4 us (7%)
  local copies, waits for them, and re-layouts  14.1 us (5%)
  starting transfers between devices  14 us (5%)
  between operations  13.3 us (4%)
    all_to_all x2, blocking collectives, mute(): lax.all_to_all(back.astype(jnp.bfloat16), 'freq', split_axis=2, concat_ax...  58.8 us
    dot_general x3, matrix products, reflect(): jnp.einsum('fasr,rbfp->safbp', reflection, field, preferred_element_type=...  52.2 us
    all_to_all x1, blocking collectives, mute(): lax.all_to_all(spectra.astype(jnp.bfloat16), 'freq', split_axis=0, concat...  32.8 us
    reduce_scatter x3, waiting for transfers between devices, reflect(): lax.psum_scatter(combine(products, signed).astype(jnp.bfloat16), 'rhalf',...  28.6 us
    all_to_all x1, waiting for transfers between devices, per_device(): lax.all_to_all(upgoing.astype(jnp.bfloat16), 'freq', split_axis=3, concat...  25.4 us
    all_to_all x1, waiting for transfers between devices, mute(): lax.all_to_all(spectra.astype(jnp.bfloat16), 'freq', split_axis=0, concat...  25.4 us
    reduce_scatter x3, local copies, waits for them, and re-layouts, reflect(): lax.psum_scatter(combine(products, signed).astype(jnp.bfloat16), 'rhalf',...  9.37 us
    add x3, other arithmetic, combine(): imag_part = products[:, 0, :, 1] + signed * products[:, 1, :, 0]  7.57 us
  transfers between devices with their start and end apart: 5, of which 5 were waited for; matrix products, arithmetic and copies ran while one was open for 0% of the time, Pallas kernels for 0%

commit v1 on v0

v1 whole, which is shorter than its diff:
```python
import math

import jax
import jax.numpy as jnp
from jax import lax
from jax.experimental import pallas as pl
from jax.experimental.pallas import tpu as pltpu
from jax.sharding import PartitionSpec as P

TILE = 512


def transform_tables(nfreq):
    ntime = 2 * nfreq
    freqs = jnp.arange(nfreq, dtype=jnp.int32)
    times = jnp.arange(ntime, dtype=jnp.int32)
    phases = freqs[:, None] * times[None, :] % ntime
    angles = phases.astype(jnp.float32) * (2.0 * math.pi / ntime)
    norm_factor = 1.0 / math.sqrt(ntime)
    weights = jnp.where(freqs == 0, 1.0, 2.0).astype(jnp.float32)[:, None] * norm_factor
    inverse = jnp.stack([weights * jnp.cos(angles), -weights * jnp.sin(angles)], axis=1)
    forward = jnp.stack([jnp.cos(angles), -jnp.sin(angles)], axis=1) * norm_factor
    return inverse.reshape(ntime, ntime), forward.reshape(ntime, ntime)


def signed_delay(ntime):
    times = jnp.arange(ntime, dtype=jnp.int32)
    return jnp.abs(jnp.where(times < ntime // 2, times, times - ntime))


def product_kernel(pieces, signed, r_ref, *refs):
    o_ref = refs[pieces]
    me = lax.axis_index("rhalf")
    freq = pl.program_id(0)
    by_real = by_imag = 0.0
    for j in range(pieces):
        x = refs[j][freq]
        rows, depth = x.shape
        owner = lax.rem(me + (pieces - j), pieces)
        at = pl.ds(pl.multiple_of(owner * depth, depth), depth)
        by_real += jnp.dot(x, r_ref[0, 0, at, :], preferred_element_type=jnp.float32)
        by_imag += jnp.dot(x, r_ref[0, 1, at, :], preferred_element_type=jnp.float32)
    half = rows // 2
    sums = (
        by_real[:half] - signed * by_imag[half:],
        by_real[half:] + signed * by_imag[:half],
    )
    if len(o_ref.shape) == 3:
        for c in range(2):
            o_ref[0, c * half : (c + 1) * half, :] = sums[c].astype(o_ref.dtype)
        return
    devices, _, _, here, tile = o_ref.shape
    for c in range(2):
        o_ref[:, 0, c] = sums[c].reshape(devices, here, tile).astype(o_ref.dtype)


def product(reflection, pieces, signed, devices):
    nf, _, full, own = reflection.shape
    _, rows, depth = pieces[0].shape
    here = rows // (2 * devices)
    tile = min(TILE, own)
    regroup = here % 8 == 0
    if regroup:
        out_shape = (devices, nf, 2, here, own)
        out_spec = pl.BlockSpec((devices, 1, 2, here, tile), lambda f, s: (0, f, 0, 0, s))
    else:
        out_shape = (nf, rows, own)
        out_spec = pl.BlockSpec((1, rows, tile), lambda f, s: (f, 0, s))
    spectra = pl.pallas_call(
        lambda *refs: product_kernel(len(pieces), signed, *refs),
        name="product_plus" if signed > 0 else "product_minus",
        out_shape=jax.ShapeDtypeStruct(out_shape, jnp.bfloat16),
        grid=(nf, own // tile),
        in_specs=[pl.BlockSpec((1, 2, full, tile), lambda f, s: (f, 0, 0, s))]
        + [pl.BlockSpec(memory_space=pltpu.VMEM) for _ in pieces],
        out_specs=out_spec,
        cost_estimate=pl.CostEstimate(
            flops=4 * nf * rows * full * own, bytes_accessed=4 * nf * full * own, transcendentals=0
        ),
    )(reflection, *pieces)
    if regroup:
        return spectra
    return jnp.transpose(spectra.reshape(nf, 2, devices, here, own), (2, 0, 1, 3, 4))


def exchange(blocks):
    return lax.all_to_all(blocks, "freq", split_axis=0, concat_axis=0, tiled=True)


def per_device(reflection, focusing_direct, arrival_index):
    own = focusing_direct.shape[0]
    freq_local = focusing_direct.shape[2]
    points = focusing_direct.shape[3]
    freq_devices = lax.axis_size("freq")
    halves = lax.axis_size("rhalf")
    nfreq = freq_local * freq_devices
    ntime = 2 * nfreq
    inverse, forward = transform_tables(nfreq)
    here = points // freq_devices
    my_index = lax.axis_index("freq")
    arrival = lax.dynamic_slice_in_dim(arrival_index, my_index * here, here, 1).T
    delay = signed_delay(ntime)
    inside = delay[:, None, None] < arrival[None]

    def reflect(field, signed):
        field = field.reshape(freq_local, 2 * points, own)
        pieces = [field]
        for shift in range(1, halves):
            pairs = [(i, (i + shift) % halves) for i in range(halves)]
            pieces.append(lax.ppermute(field, "rhalf", pairs))
        spectra = product(reflection, pieces, signed, freq_devices)
        return exchange(spectra).reshape(ntime, here, own)

    def mute(spectra):
        signal = jnp.einsum(
            "kps,kt->tps", spectra.astype(jnp.float32), inverse, precision=lax.Precision.HIGHEST
        )
        signal = jnp.where(inside, signal, 0.0)
        back = jnp.einsum("tps,kt->kps", signal, forward, precision=lax.Precision.HIGHEST)
        back = back.astype(jnp.bfloat16).reshape(freq_devices, freq_local, 2, here, own)
        back = jnp.transpose(exchange(back), (1, 2, 0, 3, 4))
        return back.reshape(freq_local, 2, points, own)

    direct = jnp.transpose(focusing_direct, (2, 1, 3, 0))
    minus = mute(reflect(direct, 1.0))
    change = mute(reflect(minus, -1.0))
    plus = (direct.astype(jnp.float32) + change.astype(jnp.float32)).astype(jnp.bfloat16)
    upgoing = reflect(plus, 1.0)
    traces = jnp.einsum(
        "kps,kt->pst", upgoing.astype(jnp.float32), inverse, precision=lax.Precision.HIGHEST
    )
    outside = delay >= arrival[:, :, None]
    return jnp.where(outside, traces, 0.0).astype(jnp.bfloat16)


def solution(mesh):
    return jax.shard_map(
        per_device,
        mesh=mesh,
        in_specs=(P("freq", None, None, "rhalf"), P("rhalf", None, "freq", None), P("rhalf", None)),
        out_specs=P("freq", "rhalf", None),
        check_vma=False,
    )
```

time: 296 us -> 211 us (0.71)
  matrix products: 61 us -> 10.3 us
  waiting for transfers between devices: 79.4 us -> 33 us
  Pallas kernels: 0 us -> 29.7 us
  blocking collectives: 91.6 us -> 120 us
  other arithmetic: 21.4 us -> 0.61 us
  between operations: 13.3 us -> 0.19 us
  local copies, waits for them, and re-layouts: 14.1 us -> 7.16 us
  starting transfers between devices: 14 us -> 7.44 us
    dot_general x8 -> x5, matrix products: 61 us -> 10.3 us  [the longest x2 4.05 us: mute(): jnp.einsum('kps,kt->tps', spectra.astype(jnp.float32), inverse, precision...]
    pallas_call x0 -> x3, Pallas kernels: none -> 29.7 us  [product(): pl.pallas_call(lambda *refs: product_kernel(len(pieces), signed, *refs),...]
    reduce_scatter x3 -> x0, waiting for transfers between devices: 28.6 us -> none  [reflect(): lax.psum_scatter(combine(products, signed).astype(jnp.bfloat16), 'rhalf',...]
    all_to_all x3 -> x4, blocking collectives: 91.6 us -> 120 us  [exchange(): lax.all_to_all(blocks, 'freq', split_axis=0, concat_axis=0, tiled=True)]
    all_to_all x2 -> x1, waiting for transfers between devices: 50.8 us -> 25.1 us  [exchange(): lax.all_to_all(blocks, 'freq', split_axis=0, concat_axis=0, tiled=True)]
    reduce_scatter x3 -> x0, local copies, waits for them, and re-layouts: 9.37 us -> none  [reflect(): lax.psum_scatter(combine(products, signed).astype(jnp.bfloat16), 'rhalf',...]
    ppermute x0 -> x3, waiting for transfers between devices: none -> 7.94 us  [reflect(): pieces.append(lax.ppermute(field, 'rhalf', pairs))]
    add x3 -> x0, other arithmetic: 7.57 us -> none  [combine(): imag_part = products[:, 0, :, 1] + signed * products[:, 1, :, 0]]
  transfers between devices with their start and end apart: 5 -> 4, of which waited for: 5 -> 4; matrix products, arithmetic and copies ran while one was open for 0% -> 0% of each run, Pallas kernels for 0% -> 0%
where the time goes in v1:
time: 211 us; the launch traced here: 208 us
  blocking collectives  120 us (57%)
  waiting for transfers between devices  33 us (16%)
  Pallas kernels  29.7 us (14%)
  matrix products  10.3 us (5%)
  starting transfers between devices  7.44 us (4%)
  local copies, waits for them, and re-layouts  7.16 us (3%)
    all_to_all x4, blocking collectives, exchange(): lax.all_to_all(blocks, 'freq', split_axis=0, concat_axis=0, tiled=True)  120 us
    pallas_call x3, Pallas kernels, product(): pl.pallas_call(lambda *refs: product_kernel(len(pieces), signed, *refs),...  29.7 us
    all_to_all x1, waiting for transfers between devices, exchange(): lax.all_to_all(blocks, 'freq', split_axis=0, concat_axis=0, tiled=True)  25.1 us
    ppermute x3, waiting for transfers between devices, reflect(): pieces.append(lax.ppermute(field, 'rhalf', pairs))  7.94 us
    all_to_all x1, starting transfers between devices, exchange(): lax.all_to_all(blocks, 'freq', split_axis=0, concat_axis=0, tiled=True)  7.22 us
    unnamed x17, local copies, waits for them, and re-layouts  5.5 us
  transfers between devices with their start and end apart: 4, of which 4 were waited for; matrix products, arithmetic and copies ran while one was open for 0% of the time, Pallas kernels for 0%

profile of v1, /device:TPU:8, one launch (start us, length us, event | category | flops | bytes accessed | tf_op | source)
XLA Modules:
  0.0 208.3 jit_solution(14773712772219332962)
XLA Ops:
  0.0 0.0 copy-start
  0.0 2.5 %copy.47 = bf16[1024,2,2,128]{0,3,1,2:T(8,128)(2,1)S(1)} copy(bf16[1024,2,2,128]{3,2,1,0:T(2,128)(2,1)} %param.4) | data formatting | bytes 2097152 | tf_op args[1]
  2.5 0.0 copy-start.1
  2.5 0.1 collective-permute-start
  2.6 2.6 %collective-permute-done.refs_2_ = bf16[2,256,1024]{2,1,0:T(8,128)(2,1)S(1)} collective-permute-done((bf16[2,256,1024]{2,1,0:T(8,128)(2,1)S(1)}, bf16[2,256,1024]{2,1,0:T(8,128)(2,1)S(1)}, u32[]{:S(2)}, u32[]{:S(2)}) %collective-permute-start) | collective-permute-done | bytes 1048608 | tf_op jit(solution)/shard_map/ppermute | solution.py:110
  5.3 0.0 copy-done.1
  5.3 0.0 copy-start.7
  5.3 1.0 copy-done.7
  6.2 9.9 %product_plus.2 = bf16[16,2,2,8,1024]{4,3,2,1,0:T(8,128)(2,1)} custom-call(bf16[2,2,2048,1024]{3,2,1,0:T(8,128)(2,1)} %refs_0_.5, bf16[2,256,1024]{2,1,0:T(8,128)(2,1)} %bitcast.34, bf16[2,256,1024]{2,1,0:T(8,128)(2,1)} %copy-done.7), custom_call_target="tpu_custom_call" | custom-call | flops 4294967296 | bytes 16777216 | tf_op jit(solution)/shard_map/product_plus/pallas_call | solution.py:69
  16.2 7.2 %all-to-all-start = ((bf16[16,2,2,8,1024]{4,3,2,1,0:T(8,128)(2,1)}), bf16[16,2,2,8,1024]{4,3,2,1,0:T(8,128)(2,1)S(1)}, u32[]{:S(2)}, u32[]{:S(2)}) async-start(bf16[16,2,2,8,1024]{4,3,2,1,0:T(8,128)(2,1)} %product_plus.2), calls=%async_computation | async-start | bytes 2097152 | tf_op jit(solution)/shard_map/all_to_all | solution.py:87
  23.4 0.1 broadcast_multiply_fusion
  23.5 0.1 fusion.23
  23.7 0.0 copy-done
  23.7 0.2 dynamic-slice_bitcast_fusion
  23.9 0.2 copy.46
  24.1 25.1 %all-to-all-done = bf16[16,2,2,8,1024]{4,3,2,1,0:T(8,128)(2,1)S(1)} async-done(((bf16[16,2,2,8,1024]{4,3,2,1,0:T(8,128)(2,1)}), bf16[16,2,2,8,1024]{4,3,2,1,0:T(8,128)(2,1)S(1)}, u32[]{:S(2)}, u32[]{:S(2)}) %all-to-all-start) | async-done | bytes 1048608 | tf_op jit(solution)/shard_map/all_to_all | solution.py:87
  49.1 2.0 fusion.8
  51.2 1.9 fusion.4
  53.1 0.6 copy.66
  53.6 29.4 %all_to_all.25 = bf16[16,2,2,8,1024]{4,3,2,1,0:T(8,128)(2,1)S(1)} all-to-all(bf16[16,2,2,8,1024]{4,3,2,1,0:T(8,128)(2,1)S(1)} %bitcast.41), channel_id=1, replica_groups=mesh['freq'=16,'rhalf'=2] {'freq'}, dimensions={0} | all-to-all | bytes 2097152 | tf_op jit(solution)/shard_map/all_to_all | solution.py:87
  83.1 0.1 copy.54
  83.2 0.0 copy-start.4
  83.2 0.1 collective-permute-start.1
  83.3 2.6 %collective-permute-done.1.refs_2_ = bf16[2,256,1024]{2,1,0:T(8,128)(2,1)S(1)} collective-permute-done((bf16[2,256,1024]{2,1,0:T(8,128)(2,1)S(1)}, bf16[2,256,1024]{2,1,0:T(8,128)(2,1)S(1)}, u32[]{:S(2)}, u32[]{:S(2)}) %collective-permute-start.1) | collective-permute-done | bytes 1048608 | tf_op jit(solution)/shard_map/ppermute | solution.py:110
  85.9 0.0 copy-done.4
  85.9 0.0 copy-start.5
  85.9 1.0 copy-done.5
  86.9 9.9 %product_minus.1 = bf16[16,2,2,8,1024]{4,3,2,1,0:T(8,128)(2,1)} custom-call(bf16[2,2,2048,1024]{3,2,1,0:T(8,128)(2,1)} %refs_0_.5, bf16[2,256,1024]{2,1,0:T(8,128)(2,1)} %bitcast.39, bf16[2,256,1024]{2,1,0:T(8,128)(2,1)} %copy-done.5), custom_call_target="tpu_custom_call" | custom-call | flops 4294967296 | bytes 16777216 | tf_op jit(solution)/shard_map/product_minus/pallas_call | solution.py:69
  96.8 30.6 %all_to_all.26 = bf16[16,2,2,8,1024]{4,3,2,1,0:T(8,128)(2,1)S(1)} all-to-all(bf16[16,2,2,8,1024]{4,3,2,1,0:T(8,128)(2,1)} %product_minus.1), channel_id=1, replica_groups=mesh['freq'=16,'rhalf'=2] {'freq'}, dimensions={0} | all-to-all | bytes 2097152 | tf_op jit(solution)/shard_map/all_to_all | solution.py:87
  127.3 2.0 fusion.6
  129.4 1.9 fusion.3
  131.3 0.0 copy-start.2
  131.3 0.6 copy.67
  131.9 29.3 %all_to_all.27 = bf16[16,2,2,8,1024]{4,3,2,1,0:T(8,128)(2,1)S(1)} all-to-all(bf16[16,2,2,8,1024]{4,3,2,1,0:T(8,128)(2,1)S(1)} %bitcast.43), channel_id=1, replica_groups=mesh['freq'=16,'rhalf'=2] {'freq'}, dimensions={0} | all-to-all | bytes 2097152 | tf_op jit(solution)/shard_map/all_to_all | solution.py:87
  161.2 0.0 copy-done.2
  161.2 0.4 fusion.2
  161.6 0.0 copy-start.3
  161.6 0.1 collective-permute-start.2
  161.7 2.6 %collective-permute-done.2.refs_2_ = bf16[2,256,1024]{2,1,0:T(8,128)(2,1)S(1)} collective-permute-done((bf16[2,256,1024]{2,1,0:T(8,128)(2,1)S(1)}, bf16[2,256,1024]{2,1,0:T(8,128)(2,1)S(1)}, u32[]{:S(2)}, u32[]{:S(2)}) %collective-permute-start.2) | collective-permute-done | bytes 1048608 | tf_op jit(solution)/shard_map/ppermute | solution.py:110
  164.3 0.0 copy-done.3
  164.3 0.0 copy-start.6
  164.3 1.0 copy-done.6
  165.3 9.9 %product_plus.3 = bf16[16,2,2,8,1024]{4,3,2,1,0:T(8,128)(2,1)} custom-call(bf16[2,2,2048,1024]{3,2,1,0:T(8,128)(2,1)} %refs_0_.5, bf16[2,256,1024]{2,1,0:T(8,128)(2,1)} %bitcast.36, bf16[2,256,1024]{2,1,0:T(8,128)(2,1)} %copy-done.6), custom_call_target="tpu_custom_call" | custom-call | flops 4294967296 | bytes 16777216 | tf_op jit(solution)/shard_map/product_plus/pallas_call | solution.py:69
  175.2 30.6 %all_to_all.28 = bf16[16,2,2,8,1024]{4,3,2,1,0:T(8,128)(2,1)S(1)} all-to-all(bf16[16,2,2,8,1024]{4,3,2,1,0:T(8,128)(2,1)} %product_plus.3), channel_id=1, replica_groups=mesh['freq'=16,'rhalf'=2] {'freq'}, dimensions={0} | all-to-all | bytes 2097152 | tf_op jit(solution)/shard_map/all_to_all | solution.py:87
  205.8 2.5 %select_convert_fusion = bf16[8,1024,64]{1,2,0:T(8,128)(2,1)} fusion(f32[64,64,1]{1,0,2:T(8,128)S(1)} %bitcast.47, bf16[64,8,1024]{2,1,0:T(8,128)(2,1)S(1)} %bitcast.44, s32[8,1024]{1,0:T(8,128)S(1)} %copy.46, s32[64]{0:T(128)S(1)} %fusion.26), kind=kOutput, calls=%fused_computation.6 | convolution fusion | flops 404226048 | bytes 2146560 | tf_op jit(solution)/shard_map/kps,kt->pst/dot_general | solution.py:129
  (7 shorter events, 0.1 us)
Async XLA Ops:
  0.0 23.7 %copy-start = (s32[1024,128]{1,0:T(8,128)S(1)}, s32[1024,128]{1,0:T(8,128)}, u32[]{:S(2)}) copy-start(s32[1024,128]{1,0:T(8,128)} %param.5) | copy-start | bytes 1572868
  2.5 2.7 %copy-start.1 = (bf16[1024,2,2,128]{0,3,1,2:T(8,128)(2,1)}, bf16[1024,2,2,128]{0,3,1,2:T(8,128)(2,1)S(1)}, u32[]{:S(2)}) copy-start(bf16[1024,2,2,128]{0,3,1,2:T(8,128)(2,1)S(1)} %copy.47) | copy-start | bytes 3145732
  2.5 2.7 %collective-permute-start = (bf16[2,256,1024]{2,1,0:T(8,128)(2,1)S(1)}, bf16[2,256,1024]{2,1,0:T(8,128)(2,1)S(1)}, u32[]{:S(2)}, u32[]{:S(2)}) collective-permute-start(bf16[2,256,1024]{2,1,0:T(8,128)(2,1)S(1)} %bitcast.33), channel_id=1, source_target_pairs={{0,1},{1,0},{2,3},{3,2},{4,5},{5,4},{6,7},{7,6},{8,9},{9,8},{10,11... | collective-permute-start | bytes 3145736 | tf_op jit(solution)/shard_map/ppermute | solution.py:110
  5.3 1.0 copy-start.7
  16.2 33.0 %all-to-all-start = ((bf16[16,2,2,8,1024]{4,3,2,1,0:T(8,128)(2,1)}), bf16[16,2,2,8,1024]{4,3,2,1,0:T(8,128)(2,1)S(1)}, u32[]{:S(2)}, u32[]{:S(2)}) async-start(bf16[16,2,2,8,1024]{4,3,2,1,0:T(8,128)(2,1)} %product_plus.2), calls=%async_computation | async-start | bytes 2097152 | tf_op jit(solution)/shard_map/all_to_all | solution.py:87
  83.2 2.7 %copy-start.4 = (bf16[2,2,16,8,1024]{4,3,2,1,0:T(8,128)(2,1)}, bf16[2,2,16,8,1024]{4,3,2,1,0:T(8,128)(2,1)S(1)}, u32[]{:S(2)}) copy-start(bf16[2,2,16,8,1024]{4,3,2,1,0:T(8,128)(2,1)S(1)} %copy.54) | copy-start | bytes 3145732
  83.2 2.7 %collective-permute-start.1 = (bf16[2,256,1024]{2,1,0:T(8,128)(2,1)S(1)}, bf16[2,256,1024]{2,1,0:T(8,128)(2,1)S(1)}, u32[]{:S(2)}, u32[]{:S(2)}) collective-permute-start(bf16[2,256,1024]{2,1,0:T(8,128)(2,1)S(1)} %bitcast.38), channel_id=1, source_target_pairs={{0,1},{1,0},{2,3},{3,2},{4,5},{5,4},{6,7},{7,6},{8,9},{9,8},{10,11... | collective-permute-start | bytes 3145736 | tf_op jit(solution)/shard_map/ppermute | solution.py:110
  85.9 1.0 copy-start.5
  131.3 29.9 %copy-start.2 = (bf16[1024,2,2,128]{0,3,1,2:T(8,128)(2,1)S(1)}, bf16[1024,2,2,128]{0,3,1,2:T(8,128)(2,1)}, u32[]{:S(2)}) copy-start(bf16[1024,2,2,128]{0,3,1,2:T(8,128)(2,1)} %copy-done.1) | copy-start | bytes 3145732
  161.6 2.7 %copy-start.3 = (bf16[2,2,128,1024]{3,2,1,0:T(8,128)(2,1)}, bf16[2,2,128,1024]{3,2,1,0:T(8,128)(2,1)S(1)}, u32[]{:S(2)}) copy-start(bf16[2,2,128,1024]{3,2,1,0:T(8,128)(2,1)S(1)} %fusion.2) | copy-start | bytes 3145732
  161.6 2.7 %collective-permute-start.2 = (bf16[2,256,1024]{2,1,0:T(8,128)(2,1)S(1)}, bf16[2,256,1024]{2,1,0:T(8,128)(2,1)S(1)}, u32[]{:S(2)}, u32[]{:S(2)}) collective-permute-start(bf16[2,256,1024]{2,1,0:T(8,128)(2,1)S(1)} %bitcast.35), channel_id=1, source_target_pairs={{0,1},{1,0},{2,3},{3,2},{4,5},{5,4},{6,7},{7,6},{8,9},{9,8},{10,11... | collective-permute-start | bytes 3145736 | tf_op jit(solution)/shard_map/ppermute | solution.py:110
  164.3 1.0 copy-start.6
